TPU v7x, 128 devices: a whole 4x4x4 slice. The times are simulated.
128 devices in a mesh: gx: 16 (over y, x), gy: 8 (over z, core).
Axes of the slice: x: 4, y: 4, z: 4, core: 2. Of those that a mesh axis runs over, the one named last changes fastest.
Arguments:
- basis: float32 [32, 256, 128, 256], P(None, 'gx', 'gy'), may hold values from -0.09375 to 0.09375
- reaction: float32 [256, 128, 256], P('gx', 'gy'), may hold values from 0.5 to 4
Outputs:
- extended: float32 [32, 256, 128, 256], P(None, 'gx', 'gy')
- coarse: float32 [128, 5, 32, 32], replicated
All inputs are finite; a program needn't handle non-finite values.
Results may differ from a plain program's by a relative error of at most 0.000071.
Values sent between devices are 32-bit elements; how exact they have to be, the bound alone decides.
No kernel may reach another device: no remote copies, remote signals or barrier semaphores. Data moves between devices by JAX's collectives and lax.ppermute only.
A program may use at most 128 MiB of HBM per device.

v0:
```python
import jax
import jax.numpy as jnp
from jax import lax
from jax.sharding import PartitionSpec as P

SWEEPS = 4
OMEGA = 0.8


def with_halo(shard, sides, width):
    edges = {}
    for axis, dim in sides:
        size, length = (lax.axis_size(axis), shard.shape[dim])
        up = [(i, (i + 1) % size) for i in range(size - 1)]
        last = lax.slice_in_dim(shard, length - width, length, axis=dim)
        first = lax.slice_in_dim(shard, 0, width, axis=dim)
        edges[dim] = (
            lax.ppermute(last, axis, up),
            lax.ppermute(first, axis, [(b, a) for a, b in up]),
        )
    done = []
    for _, dim in sides:
        low, high = edges[dim]
        around = [(width, width) if d in done else (0, 0) for d in range(shard.ndim)]
        shard = jnp.concatenate([jnp.pad(low, around), shard, jnp.pad(high, around)], axis=dim)
        done.append(dim)
    return shard


def stencil(field, coef):
    padded = jnp.pad(field, ((0, 0), (1, 1), (1, 1), (1, 1)))
    beside = padded[:, 2:, 1:-1, 1:-1] + padded[:, :-2, 1:-1, 1:-1]
    beside = beside + padded[:, 1:-1, 2:, 1:-1] + padded[:, 1:-1, :-2, 1:-1]
    beside = beside + padded[:, 1:-1, 1:-1, 2:] + padded[:, 1:-1, 1:-1, :-2]
    return (6.0 + coef) * field - beside


def couple(own, other):
    width = own.shape[0]
    return -jnp.dot(
        own.reshape(width, -1),
        other.reshape(width, -1).T,
        precision=lax.Precision.HIGHEST,
        preferred_element_type=jnp.float32,
    )


def on_device(basis, reaction):
    width, cx, cy, cz = basis.shape
    padded = with_halo(basis, (("gx", 1), ("gy", 2)), 1)
    left_face = padded[:, 0, 1:-1, :]
    right_face = padded[:, -1, 1:-1, :]
    lower_face = padded[:, 1:-1, 0, :]
    upper_face = padded[:, 1:-1, -1, :]
    xpos = lax.broadcasted_iota(jnp.int32, (cx, cy, cz), 0)
    ypos = lax.broadcasted_iota(jnp.int32, (cx, cy, cz), 1)
    inner = (xpos >= 1) & (xpos <= cx - 2) & (ypos >= 1) & (ypos <= cy - 2)
    phi = basis
    for sweep in range(SWEEPS):
        update = OMEGA * stencil(phi, reaction) / (6.0 + reaction)
        phi = phi - jnp.where(inner[None], update, jnp.float32(0.0))
    applied = stencil(phi, reaction)
    diag = jnp.dot(
        phi.reshape(width, -1),
        applied.reshape(width, -1).T,
        precision=lax.Precision.HIGHEST,
        preferred_element_type=jnp.float32,
    )
    blocks = jnp.stack(
        [
            diag,
            couple(basis[:, 0], left_face),
            couple(basis[:, -1], right_face),
            couple(basis[:, :, 0], lower_face),
            couple(basis[:, :, -1], upper_face),
        ]
    )
    coarse = lax.all_gather(blocks[None], ("gx", "gy"), axis=0, tiled=True)
    return (phi, coarse)


def solution(mesh):
    placed = (P(None, "gx", "gy", None), P("gx", "gy", None))
    return jax.shard_map(
        on_device,
        mesh=mesh,
        in_specs=placed,
        out_specs=(P(None, "gx", "gy", None), P()),
        check_vma=False,
    )
```

profile of v0, /device:TPU:1, one launch (start us, length us, event | category | flops | bytes accessed | tf_op | source)
XLA Modules:
  0.0 217.7 jit_solution(16846393999798236059)
XLA Ops:
  7.2 0.0 all-gather.3.cloned.1.call-start
  7.2 0.0 copy-start.1
  7.2 1.4 fusion.77
  8.7 1.1 copy.20
  9.8 4.9 %collective-permute-start = (f32[32,1,16,256]{3,0,2,1:T(8,128)}, f32[32,1,16,256]{3,0,2,1:T(8,128)}, u32[]{:S(2)}, u32[]{:S(2)}) collective-permute-start(f32[32,1,16,256]{3,0,2,1:T(8,128)} %copy.20), channel_id=1, source_target_pairs={{0,8},{8,16},{16,24},{24,32},{32,40},{40,48},{48,56},{56,64},{64,7... | collective-permute-start | bytes 1572872 | tf_op jit(solution)/shard_map/ppermute | solution.py:18
  14.6 1.1 copy.19
  15.8 1.3 collective-permute-start.1
  17.1 4.4 %fusion.76 = (f32[32,16,1,256]{3,2,1,0:T(1,128)S(1)}, f32[32,16,1,256]{3,2,1,0:T(1,128)S(1)}) fusion(f32[32,16,16,256]{3,2,1,0:T(8,128)} %param.2), kind=kLoop, calls=%fused_computation.110 | loop fusion | bytes 2097152 | tf_op jit(solution)/shard_map/slice | solution.py:74
  21.5 1.1 copy.22
  22.6 4.4 %collective-permute-start.2 = (f32[32,16,1,256]{3,0,1,2:T(8,128)}, f32[32,16,1,256]{3,0,1,2:T(8,128)}, u32[]{:S(2)}, u32[]{:S(2)}) collective-permute-start(f32[32,16,1,256]{3,0,1,2:T(8,128)} %copy.22), channel_id=1, source_target_pairs={{0,1},{1,2},{2,3},{3,4},{4,5},{5,6},{6,7},{8,9},{9,10},{10,11},{11... | collective-permute-start | bytes 1572872 | tf_op jit(solution)/shard_map/ppermute | solution.py:18
  27.0 1.1 copy.21
  28.1 2.1 collective-permute-start.3
  30.2 1.0 broadcast_add_fusion
  31.2 0.1 and_and_fusion
  31.3 0.0 copy-done.1
  31.3 9.6 %select_subtract_fusion.3 = f32[32,16,16,256]{3,2,1,0:T(8,128)} fusion(f32[32,16,16,256]{3,2,1,0:T(8,128)S(1)} %copy-done.1, f32[16,16,256]{2,1,0:T(8,128)S(1)} %broadcast_add_fusion, pred[16,16,256]{2,1,0:T(8,128)(4,1)S(1)} %and_and_fusion), kind=kLoop, calls=%fused_computation.74 | loop fusion | flops 23068672 | bytes 17104896 | tf_op jit(solution)/shard_map/sub | solution.py:61
  40.9 21.9 %select_subtract_fusion.2 = f32[32,16,16,256]{3,2,1,0:T(8,128)S(1)} fusion(f32[32,16,16,256]{3,2,1,0:T(8,128)} %select_subtract_fusion.3, f32[16,16,256]{2,1,0:T(8,128)S(1)} %broadcast_add_fusion, pred[16,16,256]{2,1,0:T(8,128)(4,1)S(1)} %and_and_fusion), kind=kLoop, calls=%fused_computation.73 | loop fusion | flops 23068672 | bytes 17104896 | tf_op jit(solution)/shard_map/sub | solution.py:61
  62.8 9.6 %select_subtract_fusion.1 = f32[32,16,16,256]{3,2,1,0:T(8,128)} fusion(f32[32,16,16,256]{3,2,1,0:T(8,128)S(1)} %select_subtract_fusion.2, f32[16,16,256]{2,1,0:T(8,128)S(1)} %broadcast_add_fusion, pred[16,16,256]{2,1,0:T(8,128)(4,1)S(1)} %and_and_fusion), kind=kLoop, calls=%fused_computation.72 | loop fusion | flops 23068672 | bytes 17104896 | tf_op jit(solution)/shard_map/sub | solution.py:61
  72.4 21.9 %select_subtract_fusion = f32[32,16,16,256]{3,2,1,0:T(8,128)S(1)} fusion(f32[32,16,16,256]{3,2,1,0:T(8,128)} %select_subtract_fusion.1, f32[16,16,256]{2,1,0:T(8,128)S(1)} %broadcast_add_fusion, pred[16,16,256]{2,1,0:T(8,128)(4,1)S(1)} %and_and_fusion), kind=kLoop, calls=%fused_computation.71 | loop fusion | flops 23068672 | bytes 17104896 | tf_op jit(solution)/shard_map/sub | solution.py:61
  94.3 0.0 copy-start
  94.3 9.3 %fusion.37 = f32[32,16,16,256]{3,2,1,0:T(8,128)} fusion(f32[32,16,16,256]{3,2,1,0:T(8,128)S(1)} %select_subtract_fusion, f32[16,16,256]{2,1,0:T(8,128)S(1)} %broadcast_add_fusion), kind=kLoop, calls=%fused_computation.67 | loop fusion | flops 14680064 | bytes 17039360 | tf_op jit(solution)/shard_map/sub | solution.py:35
  103.6 0.0 copy-done
  103.6 16.2 %fusion.58 = f32[5,32,32]{2,1,0:T(8,128)S(1)} fusion(f32[32,16,16,256]{3,2,1,0:T(8,128)} %fusion.37, f32[32,16,16,256]{3,2,1,0:T(8,128)S(1)} %select_subtract_fusion), kind=kOutput, calls=%fused_computation.92 | convolution fusion | flops 805306368 | bytes 16793600 | tf_op jit(solution)/shard_map/dot_general | solution.py:63
  119.8 0.0 collective-permute-done
  119.8 1.9 fusion.52
  121.7 0.0 collective-permute-done.1
  121.7 1.9 fusion.49
  123.6 0.0 collective-permute-done.2
  123.6 1.9 fusion.46
  125.5 0.0 collective-permute-done.3
  125.5 0.8 fusion.43
  126.3 0.0 copy-start.2
  126.3 0.6 copy-done.2
  127.0 0.0 all-gather.3.cloned.1.call-update
  127.0 74.6 %all-gather.3.cloned.1.call-done = f32[640,32,32]{2,1,0:T(8,128)} async-done(((f32[5,32,32]{2,1,0:T(8,128)}), f32[640,32,32]{2,1,0:T(8,128)}) %all-gather.3.cloned.1.call-update) | async-done | bytes 2621456 | tf_op jit(solution)/shard_map/all_gather | solution.py:78
  201.6 9.2 %copy.17 = f32[128,5,32,32]{0,3,2,1:T(8,128)} copy(f32[128,5,32,32]{3,2,1,0:T(8,128)} %bitcast.81) | data formatting | bytes 5242880
  (2 shorter events, 0.0 us)
Async XLA Ops:
  7.2 194.4 %all-gather.3.cloned.1.call-start = ((), (), s32[]{:S(2)}) async-start(), calls=%async_computation | async-start | bytes 10567680 | tf_op jit(solution)/shard_map/all_gather | solution.py:78
  7.2 24.1 %copy-start.1 = (f32[32,16,16,256]{3,2,1,0:T(8,128)S(1)}, f32[32,16,16,256]{3,2,1,0:T(8,128)}, u32[]{:S(2)}) copy-start(f32[32,16,16,256]{3,2,1,0:T(8,128)} %param.2) | copy-start | bytes 25165828
  9.8 110.1 %collective-permute-start = (f32[32,1,16,256]{3,0,2,1:T(8,128)}, f32[32,1,16,256]{3,0,2,1:T(8,128)}, u32[]{:S(2)}, u32[]{:S(2)}) collective-permute-start(f32[32,1,16,256]{3,0,2,1:T(8,128)} %copy.20), channel_id=1, source_target_pairs={{0,8},{8,16},{16,24},{24,32},{32,40},{40,48},{48,56},{56,64},{64,7... | collective-permute-start | bytes 1572872 | tf_op jit(solution)/shard_map/ppermute | solution.py:18
  15.8 105.9 %collective-permute-start.1 = (f32[32,1,16,256]{3,0,2,1:T(8,128)}, f32[32,1,16,256]{3,0,2,1:T(8,128)}, u32[]{:S(2)}, u32[]{:S(2)}) collective-permute-start(f32[32,1,16,256]{3,0,2,1:T(8,128)} %copy.19), channel_id=1, source_target_pairs={{8,0},{16,8},{24,16},{32,24},{40,32},{48,40},{56,48},{64,56},{72,6... | collective-permute-start | bytes 1572872 | tf_op jit(solution)/shard_map/ppermute | solution.py:19
  22.6 101.0 %collective-permute-start.2 = (f32[32,16,1,256]{3,0,1,2:T(8,128)}, f32[32,16,1,256]{3,0,1,2:T(8,128)}, u32[]{:S(2)}, u32[]{:S(2)}) collective-permute-start(f32[32,16,1,256]{3,0,1,2:T(8,128)} %copy.22), channel_id=1, source_target_pairs={{0,1},{1,2},{2,3},{3,4},{4,5},{5,6},{6,7},{8,9},{9,10},{10,11},{11... | collective-permute-start | bytes 1572872 | tf_op jit(solution)/shard_map/ppermute | solution.py:18
  28.1 97.4 %collective-permute-start.3 = (f32[32,16,1,256]{3,0,1,2:T(8,128)}, f32[32,16,1,256]{3,0,1,2:T(8,128)S(1)}, u32[]{:S(2)}, u32[]{:S(2)}) collective-permute-start(f32[32,16,1,256]{3,0,1,2:T(8,128)} %copy.21), channel_id=1, source_target_pairs={{1,0},{2,1},{3,2},{4,3},{5,4},{6,5},{7,6},{9,8},{10,9},{11,10},{12... | collective-permute-start | bytes 1572872 | tf_op jit(solution)/shard_map/ppermute | solution.py:19
  94.3 9.3 %copy-start = (f32[32,16,16,256]{3,2,1,0:T(8,128)}, f32[32,16,16,256]{3,2,1,0:T(8,128)S(1)}, u32[]{:S(2)}) copy-start(f32[32,16,16,256]{3,2,1,0:T(8,128)S(1)} %select_subtract_fusion) | copy-start | bytes 25165828
  126.3 0.6 copy-start.2
Sparse Core Ops, SparseCore 0:
  127.1 74.4 all-gather.2
where the time goes:
time: 218 us
  waiting for transfers between devices  74.6 us (34%)
  other arithmetic  73.3 us (34%)
  matrix products  22.7 us (10%)
  local copies, waits for them, and re-layouts  20.2 us (9%)
  between operations  14.2 us (7%)
  starting transfers between devices  12.7 us (6%)
    all_gather x1, waiting for transfers between devices, on_device(): coarse = lax.all_gather(blocks[None], ('gx', 'gy'), axis=0, tiled=True)  74.6 us
    sub x4, other arithmetic, on_device(): phi = phi - jnp.where(inner[None], update, jnp.float32(0.0))  63 us
    dot_general x1, matrix products, on_device(): jnp.dot(phi.reshape(width, -1), applied.reshape(width, -1).T, precision=l...  16.2 us
    unnamed x11, local copies, waits for them, and re-layouts  14.3 us
    sub x1, other arithmetic, stencil(): return (6.0 + coef) * field - beside  9.28 us
    ppermute x2, starting transfers between devices, with_halo(): lax.ppermute(last, axis, up)  9.26 us
    dot_general x4, matrix products, couple(): jnp.dot(own.reshape(width, -1), other.reshape(width, -1).T, precision=lax...  6.45 us
    slice x1, local copies, waits for them, and re-layouts, on_device(): basis[:, :, 0]  4.41 us
  transfers between devices with their start and end apart: 5, of which 1 were waited for; matrix products, arithmetic and copies ran while one was open for 47% of the time, Pallas kernels for 0%

commit v1 on v0

--- a/solution.py
+++ b/solution.py
@@ -75,7 +75,10 @@
             couple(basis[:, :, -1], upper_face),
         ]
     )
-    coarse = lax.all_gather(blocks[None], ("gx", "gy"), axis=0, tiled=True)
+    coarse = jnp.concatenate(
+        lax.all_to_all(jnp.stack([blocks[None]] * lax.axis_size(("gx", "gy"))), ("gx", "gy"), 0, 0),
+        axis=0,
+    )
     return (phi, coarse)
 
 

time: 218 us -> 208 us (0.954)
  waiting for transfers between devices: 74.6 us -> 0.01 us
  blocking collectives: 0 us -> 46.5 us
  local copies, waits for them, and re-layouts: 20.2 us -> 42.1 us
  between operations: 14.2 us -> 0.81 us
  other arithmetic: 73.3 us -> 82.4 us
    all_gather x1 -> x0, waiting for transfers between devices: 74.6 us -> none  [on_device(): coarse = lax.all_gather(blocks[None], ('gx', 'gy'), axis=0, tiled=True)]
    all_to_all x0 -> x1, blocking collectives: none -> 46.5 us  [on_device(): lax.all_to_all(jnp.stack([blocks[None]] * lax.axis_size(('gx', 'gy'))), (...]
    unnamed x11, local copies, waits for them, and re-layouts: 14.3 us -> 30.3 us
    all_to_all x0 -> x1, other arithmetic: none -> 9.11 us  [on_device(): lax.all_to_all(jnp.stack([blocks[None]] * lax.axis_size(('gx', 'gy'))), (...]
    another operation x0 -> x1, local copies, waits for them, and re-layouts: none -> 5.31 us  [on_device(): jnp.stack([blocks[None]] * lax.axis_size(('gx', 'gy')))]
  transfers between devices with their start and end apart: 5 -> 4, of which waited for: 1 -> 0; matrix products, arithmetic and copies ran while one was open for 47% -> 50% of each run, Pallas kernels for 0% -> 0%
where the time goes in v1:
time: 208 us; the launch traced here: 207 us
  other arithmetic  82.4 us (40%)
  blocking collectives  46.5 us (22%)
  local copies, waits for them, and re-layouts  42.1 us (20%)
  matrix products  22.7 us (11%)
  starting transfers between devices  12.6 us (6%)
    sub x4, other arithmetic, on_device(): phi = phi - jnp.where(inner[None], update, jnp.float32(0.0))  63 us
    all_to_all x1, blocking collectives, on_device(): lax.all_to_all(jnp.stack([blocks[None]] * lax.axis_size(('gx', 'gy'))), (...  46.5 us
    unnamed x11, local copies, waits for them, and re-layouts  30.3 us
    dot_general x1, matrix products, on_device(): jnp.dot(phi.reshape(width, -1), applied.reshape(width, -1).T, precision=l...  16.2 us
    ppermute x2, starting transfers between devices, with_halo(): lax.ppermute(last, axis, up)  9.27 us
    sub x1, other arithmetic, stencil(): return (6.0 + coef) * field - beside  9.2 us
    all_to_all x1, other arithmetic, on_device(): lax.all_to_all(jnp.stack([blocks[None]] * lax.axis_size(('gx', 'gy'))), (...  9.11 us
    dot_general x4, matrix products, couple(): jnp.dot(own.reshape(width, -1), other.reshape(width, -1).T, precision=lax...  6.45 us
  transfers between devices with their start and end apart: 4, of which 0 were waited for; matrix products, arithmetic and copies ran while one was open for 50% of the time, Pallas kernels for 0%

profile of v1, /device:TPU:1, one launch (start us, length us, event | category | flops | bytes accessed | tf_op | source)
XLA Modules:
  0.0 207.1 jit_solution(14396473811292391515)
XLA Ops:
  0.6 0.0 copy-start.1
  0.6 1.4 fusion.77
  2.1 1.1 copy.19
  3.2 4.9 %collective-permute-start = (f32[32,1,16,256]{3,0,2,1:T(8,128)}, f32[32,1,16,256]{3,0,2,1:T(8,128)}, u32[]{:S(2)}, u32[]{:S(2)}) collective-permute-start(f32[32,1,16,256]{3,0,2,1:T(8,128)} %copy.19), channel_id=1, source_target_pairs={{0,8},{8,16},{16,24},{24,32},{32,40},{40,48},{48,56},{56,64},{64,7... | collective-permute-start | bytes 1572872 | tf_op jit(solution)/shard_map/ppermute | solution.py:18
  8.1 1.1 copy.18
  9.2 1.3 collective-permute-start.1
  10.5 4.4 %fusion.76 = (f32[32,16,1,256]{3,2,1,0:T(1,128)S(1)}, f32[32,16,1,256]{3,2,1,0:T(1,128)S(1)}) fusion(f32[32,16,16,256]{3,2,1,0:T(8,128)} %param.2), kind=kLoop, calls=%fused_computation.110 | loop fusion | bytes 2097152 | tf_op jit(solution)/shard_map/slice | solution.py:74
  14.9 1.1 copy.21
  16.0 4.4 %collective-permute-start.2 = (f32[32,16,1,256]{3,0,1,2:T(8,128)}, f32[32,16,1,256]{3,0,1,2:T(8,128)}, u32[]{:S(2)}, u32[]{:S(2)}) collective-permute-start(f32[32,16,1,256]{3,0,1,2:T(8,128)} %copy.21), channel_id=1, source_target_pairs={{0,1},{1,2},{2,3},{3,4},{4,5},{5,6},{6,7},{8,9},{9,10},{10,11},{11... | collective-permute-start | bytes 1572872 | tf_op jit(solution)/shard_map/ppermute | solution.py:18
  20.4 1.1 copy.20
  21.5 2.1 %collective-permute-start.3 = (f32[32,16,1,256]{3,0,1,2:T(8,128)}, f32[32,16,1,256]{3,0,1,2:T(8,128)S(1)}, u32[]{:S(2)}, u32[]{:S(2)}) collective-permute-start(f32[32,16,1,256]{3,0,1,2:T(8,128)} %copy.20), channel_id=1, source_target_pairs={{1,0},{2,1},{3,2},{4,3},{5,4},{6,5},{7,6},{9,8},{10,9},{11,10},{12... | collective-permute-start | bytes 1572872 | tf_op jit(solution)/shard_map/ppermute | solution.py:19
  23.6 1.0 broadcast_add_fusion
  24.6 0.1 and_and_fusion
  24.7 0.0 copy-done.1
  24.7 9.6 %select_subtract_fusion.3 = f32[32,16,16,256]{3,2,1,0:T(8,128)} fusion(f32[32,16,16,256]{3,2,1,0:T(8,128)S(1)} %copy-done.1, f32[16,16,256]{2,1,0:T(8,128)S(1)} %broadcast_add_fusion, pred[16,16,256]{2,1,0:T(8,128)(4,1)S(1)} %and_and_fusion), kind=kLoop, calls=%fused_computation.74 | loop fusion | flops 23068672 | bytes 17104896 | tf_op jit(solution)/shard_map/sub | solution.py:61
  34.3 21.9 %select_subtract_fusion.2 = f32[32,16,16,256]{3,2,1,0:T(8,128)S(1)} fusion(f32[32,16,16,256]{3,2,1,0:T(8,128)} %select_subtract_fusion.3, f32[16,16,256]{2,1,0:T(8,128)S(1)} %broadcast_add_fusion, pred[16,16,256]{2,1,0:T(8,128)(4,1)S(1)} %and_and_fusion), kind=kLoop, calls=%fused_computation.73 | loop fusion | flops 23068672 | bytes 17104896 | tf_op jit(solution)/shard_map/sub | solution.py:61
  56.2 9.6 %select_subtract_fusion.1 = f32[32,16,16,256]{3,2,1,0:T(8,128)} fusion(f32[32,16,16,256]{3,2,1,0:T(8,128)S(1)} %select_subtract_fusion.2, f32[16,16,256]{2,1,0:T(8,128)S(1)} %broadcast_add_fusion, pred[16,16,256]{2,1,0:T(8,128)(4,1)S(1)} %and_and_fusion), kind=kLoop, calls=%fused_computation.72 | loop fusion | flops 23068672 | bytes 17104896 | tf_op jit(solution)/shard_map/sub | solution.py:61
  65.8 21.9 %select_subtract_fusion = f32[32,16,16,256]{3,2,1,0:T(8,128)S(1)} fusion(f32[32,16,16,256]{3,2,1,0:T(8,128)} %select_subtract_fusion.1, f32[16,16,256]{2,1,0:T(8,128)S(1)} %broadcast_add_fusion, pred[16,16,256]{2,1,0:T(8,128)(4,1)S(1)} %and_and_fusion), kind=kLoop, calls=%fused_computation.71 | loop fusion | flops 23068672 | bytes 17104896 | tf_op jit(solution)/shard_map/sub | solution.py:61
  87.7 0.0 copy-start
  87.7 9.2 %fusion.37 = f32[32,16,16,256]{3,2,1,0:T(8,128)} fusion(f32[32,16,16,256]{3,2,1,0:T(8,128)S(1)} %select_subtract_fusion, f32[16,16,256]{2,1,0:T(8,128)S(1)} %broadcast_add_fusion), kind=kLoop, calls=%fused_computation.67 | loop fusion | flops 14680064 | bytes 17039360 | tf_op jit(solution)/shard_map/sub | solution.py:35
  96.9 0.0 copy-done
  96.9 16.2 %fusion.58 = f32[5,32,32]{2,1,0:T(8,128)S(1)} fusion(f32[32,16,16,256]{3,2,1,0:T(8,128)} %fusion.37, f32[32,16,16,256]{3,2,1,0:T(8,128)S(1)} %select_subtract_fusion), kind=kOutput, calls=%fused_computation.92 | convolution fusion | flops 805306368 | bytes 16793600 | tf_op jit(solution)/shard_map/dot_general | solution.py:63
  113.2 0.0 collective-permute-done
  113.2 1.9 fusion.52
  115.0 0.0 collective-permute-done.1
  115.1 1.9 fusion.49
  116.9 0.0 collective-permute-done.2
  117.0 1.9 fusion.46
  118.8 0.0 collective-permute-done.3
  118.8 0.8 fusion.43
  119.7 5.3 %stack.27 = f32[128,1,5,32,32]{4,3,2,1,0:T(8,128)} broadcast(f32[5,32,32]{2,1,0:T(8,128)S(1)} %fusion.43), dimensions={2,3,4} | broadcast | bytes 2641920 | tf_op jit(solution)/shard_map/stack | solution.py:79
  125.0 9.3 %reshape.52 = f32[128,1,5120]{2,1,0:T(1,128)} reshape(f32[128,1,5,32,32]{4,3,2,1,0:T(8,128)} %stack.27) | data formatting | bytes 5242880
  134.2 46.5 %all_to_all.5 = f32[128,1,5120]{2,1,0:T(1,128)S(1)} all-to-all(f32[128,1,5120]{2,1,0:T(1,128)} %reshape.52), channel_id=1, replica_groups=mesh['gx'=16,'gy'=8] {'gx','gy'}, dimensions={0} | all-to-all | bytes 5242880 | tf_op jit(solution)/shard_map/all_to_all | solution.py:79
  180.8 0.6 broadcast.62
  181.4 9.1 %reduce = f32[128,5120]{1,0:T(8,128)} reduce(f32[128,1,5120]{2,1,0:T(1,128)S(1)} %all_to_all.5, f32[]{:T(128)} %broadcast.62), dimensions={1}, to_apply=%all_to_all.3.reduce_sub_computation | reduce | bytes 5242884 | tf_op jit(solution)/shard_map/all_to_all | solution.py:79
  190.5 7.4 %reshape.53 = f32[128,1,5,32,32]{4,3,2,1,0:T(8,128)} reshape(f32[128,5120]{1,0:T(8,128)} %reduce) | data formatting | bytes 5242880
  197.8 9.2 %copy.16 = f32[128,5,32,32]{0,3,2,1:T(8,128)} copy(f32[128,5,32,32]{3,2,1,0:T(8,128)} %bitcast.81) | data formatting | bytes 5242880
  (2 shorter events, 0.0 us)
Async XLA Ops:
  0.6 24.1 %copy-start.1 = (f32[32,16,16,256]{3,2,1,0:T(8,128)S(1)}, f32[32,16,16,256]{3,2,1,0:T(8,128)}, u32[]{:S(2)}) copy-start(f32[32,16,16,256]{3,2,1,0:T(8,128)} %param.2) | copy-start | bytes 25165828
  3.2 110.0 %collective-permute-start = (f32[32,1,16,256]{3,0,2,1:T(8,128)}, f32[32,1,16,256]{3,0,2,1:T(8,128)}, u32[]{:S(2)}, u32[]{:S(2)}) collective-permute-start(f32[32,1,16,256]{3,0,2,1:T(8,128)} %copy.19), channel_id=1, source_target_pairs={{0,8},{8,16},{16,24},{24,32},{32,40},{40,48},{48,56},{56,64},{64,7... | collective-permute-start | bytes 1572872 | tf_op jit(solution)/shard_map/ppermute | solution.py:18
  9.2 105.8 %collective-permute-start.1 = (f32[32,1,16,256]{3,0,2,1:T(8,128)}, f32[32,1,16,256]{3,0,2,1:T(8,128)}, u32[]{:S(2)}, u32[]{:S(2)}) collective-permute-start(f32[32,1,16,256]{3,0,2,1:T(8,128)} %copy.18), channel_id=1, source_target_pairs={{8,0},{16,8},{24,16},{32,24},{40,32},{48,40},{56,48},{64,56},{72,6... | collective-permute-start | bytes 1572872 | tf_op jit(solution)/shard_map/ppermute | solution.py:19
  16.0 100.9 %collective-permute-start.2 = (f32[32,16,1,256]{3,0,1,2:T(8,128)}, f32[32,16,1,256]{3,0,1,2:T(8,128)}, u32[]{:S(2)}, u32[]{:S(2)}) collective-permute-start(f32[32,16,1,256]{3,0,1,2:T(8,128)} %copy.21), channel_id=1, source_target_pairs={{0,1},{1,2},{2,3},{3,4},{4,5},{5,6},{6,7},{8,9},{9,10},{10,11},{11... | collective-permute-start | bytes 1572872 | tf_op jit(solution)/shard_map/ppermute | solution.py:18
  21.5 97.3 %collective-permute-start.3 = (f32[32,16,1,256]{3,0,1,2:T(8,128)}, f32[32,16,1,256]{3,0,1,2:T(8,128)S(1)}, u32[]{:S(2)}, u32[]{:S(2)}) collective-permute-start(f32[32,16,1,256]{3,0,1,2:T(8,128)} %copy.20), channel_id=1, source_target_pairs={{1,0},{2,1},{3,2},{4,3},{5,4},{6,5},{7,6},{9,8},{10,9},{11,10},{12... | collective-permute-start | bytes 1572872 | tf_op jit(solution)/shard_map/ppermute | solution.py:19
  87.7 9.2 %copy-start = (f32[32,16,16,256]{3,2,1,0:T(8,128)}, f32[32,16,16,256]{3,2,1,0:T(8,128)S(1)}, u32[]{:S(2)}) copy-start(f32[32,16,16,256]{3,2,1,0:T(8,128)S(1)} %select_subtract_fusion) | copy-start | bytes 25165828
